TPU v7x, 32 devices: a whole 2x2x4 slice. The times are simulated.
32 devices in a mesh: gx: 4 (over z), gy: 4 (over y, x), gz: 2 (over core).
Axes of the slice: x: 2, y: 2, z: 4, core: 2. Of those that a mesh axis runs over, the one named last changes fastest.
Arguments:
- test_vectors: float32 [8, 64, 64, 2048], P(None, 'gx', 'gy', 'gz'), as said below
- aniso: int32 [3, 2], replicated, may hold values from 2 to 4
Outputs:
- basis: float32 [8, 64, 64, 2048], P(None, 'gx', 'gy', 'gz')
- coarse_basis: float32 [8, 32, 32, 1024], P(None, 'gx', 'gy', 'gz')
Inputs may be any that keep to these rules, and one draw needn't show every extreme that they name: `test_vectors`: positive and negative values; every test vector is linearly independent of the others.
All inputs are finite; a program needn't handle non-finite values.
Results may differ from a plain program's by a relative error of at most 0.00029.
Values sent between devices are 32-bit elements; how exact they have to be, the bound alone decides.
A program may use at most 384 MiB of HBM per device.

v0:
```python
import jax
import jax.numpy as jnp
from jax import lax
from jax.sharding import PartitionSpec as P

SWEEPS = 3


omega_weight = 2.0 / 3.0


def extended(block, sides, width):
    for axis, dim in sides:
        count = lax.axis_size(axis)
        forward = [(i, i + 1) for i in range(count - 1)]
        backward = [(target, source) for source, target in forward]
        low = lax.ppermute(
            lax.slice_in_dim(block, block.shape[dim] - width, None, axis=dim), axis, forward
        )
        high = lax.ppermute(lax.slice_in_dim(block, 0, width, axis=dim), axis, backward)
        block = jnp.concatenate([low, block, high], axis=dim)
    return block


def jacobi_sweep(padded, coefficients, scaled):
    center = padded[:, 1:-1, 1:-1, 1:-1]
    beside = coefficients[0] * (padded[:, 2:, 1:-1, 1:-1] + padded[:, :-2, 1:-1, 1:-1])
    beside = beside + coefficients[1] * (padded[:, 1:-1, 2:, 1:-1] + padded[:, 1:-1, :-2, 1:-1])
    beside = beside + coefficients[2] * (padded[:, 1:-1, 1:-1, 2:] + padded[:, 1:-1, 1:-1, :-2])
    return (1.0 - omega_weight) * center + scaled * beside


def single_sweep(fields, coefficients, scaled):
    padded = extended(fields, (("gx", 1), ("gy", 2), ("gz", 3)), 1)
    return jacobi_sweep(padded, coefficients, scaled)


def orthonormal(gram_total, data):
    lower_factor = jnp.linalg.cholesky(gram_total)
    eye_matrix = jnp.eye(gram_total.shape[0], dtype=gram_total.dtype)
    inverse = jax.scipy.linalg.solve_triangular(lower_factor, eye_matrix, lower=True)
    return jnp.einsum("kl,lxyz->kxyz", inverse, data, precision=lax.Precision.HIGHEST)


def local(test_vectors, aniso):
    coefficients = aniso[:, 0].astype(jnp.float32) / aniso[:, 1].astype(jnp.float32)
    scaled = omega_weight / (2.0 * (coefficients[0] + coefficients[1] + coefficients[2]))
    vectors, rows_x, rows_y, rows_z = test_vectors.shape
    fields = test_vectors
    for sweep_index in range(SWEEPS):
        fields = single_sweep(fields, coefficients, scaled)
    flattened = fields.reshape(vectors, -1)
    gram_part = jnp.dot(flattened, flattened.T, precision=lax.Precision.HIGHEST)
    coarse = fields.reshape(vectors, rows_x // 2, 2, rows_y // 2, 2, rows_z // 2, 2).mean(
        axis=(2, 4, 6)
    )
    coarse_flat = coarse.reshape(vectors, -1)
    coarse_part = jnp.dot(coarse_flat, coarse_flat.T, precision=lax.Precision.HIGHEST)
    gram_total, coarse_gram = lax.psum((gram_part, coarse_part), ("gx", "gy", "gz"))
    cell_count = (
        rows_x * rows_y * rows_z * lax.axis_size("gx") * lax.axis_size("gy") * lax.axis_size("gz")
    )
    gram_total = gram_total / cell_count
    coarse_gram = coarse_gram / (cell_count // 8)
    return (orthonormal(gram_total, fields), orthonormal(coarse_gram, coarse))


def solution(mesh):
    placed = (P(None, "gx", "gy", "gz"), P())
    return jax.shard_map(
        local,
        mesh=mesh,
        in_specs=placed,
        out_specs=(P(None, "gx", "gy", "gz"), P(None, "gx", "gy", "gz")),
        check_vma=False,
    )
```

profile of v0, /device:TPU:0, one launch (start us, length us, event | category | flops | bytes accessed | tf_op | source)
XLA Modules:
  0.0 622.9 jit_solution(8124295138324936819)
XLA Ops:
  0.6 10.1 %copy.57 = f32[8,16,16,1024]{3,0,2,1:T(8,128)S(1)} copy(f32[8,16,16,1024]{3,2,1,0:T(8,128)} %param.5) | data formatting | bytes 16777216 | tf_op args[0]
  10.8 5.0 collective-permute-start.1
  15.8 1.5 collective-permute-start
  17.3 9.6 %collective-permute-done.1 = f32[8,1,16,1024]{3,0,2,1:T(8,128)S(1)} collective-permute-done((f32[8,1,16,1024]{3,0,2,1:T(8,128)S(1)}, f32[8,1,16,1024]{3,0,2,1:T(8,128)S(1)}, u32[]{:S(2)}, u32[]{:S(2)}) %collective-permute-start.1) | collective-permute-done | bytes 524320 | tf_op jit(solution)/shard_map/ppermute | solution.py:17
  27.8 7.1 %constant_dynamic-update-slice_fusion.1 = f32[8,18,16,1024]{3,0,2,1:T(8,128)S(1)} fusion(f32[8,18,16,1024]{3,0,2,1:T(8,128)S(1)} %constant_dynamic-update-slice_fusion.2, f32[8,16,16,1024]{3,2,1,0:T(8,128)S(1)} %copy-done.4), kind=kLoop, calls=%fused_computation.104 | loop fusion | bytes 16777216
  35.2 1.3 collective-permute-start.2
  36.5 4.6 collective-permute-start.3
  41.1 12.2 %collective-permute-done.2 = f32[8,18,1,1024]{3,0,2,1:T(8,128)S(1)} collective-permute-done((f32[8,18,1,1024]{3,0,2,1:T(8,128)S(1)}, f32[8,18,1,1024]{3,0,2,1:T(8,128)S(1)}, u32[]{:S(2)}, u32[]{:S(2)}) %collective-permute-start.2) | collective-permute-done | bytes 589856 | tf_op jit(solution)/shard_map/ppermute | solution.py:20
  57.3 3.2 collective-permute-start.5
  65.0 29.0 %fusion.24 = f32[8,16,16,1024]{3,0,2,1:T(8,128)S(1)} fusion(f32[8,18,18,1]{3,0,2,1:T(8,128)S(1)} %copy.66, f32[8,18,1,1024]{3,0,2,1:T(8,128)S(1)} %collective-permute-done.2, f32[8,18,16,1024]{3,0,2,1:T(8,128)} %copy-done.2, f32[8,18,1,1024]{3,0,2,1:T(8,128)} %copy-done.11, f32[8,18,18,1]{3,0,2,1:T(8,128)S(1)} %copy.64, f32[8,16,16,1024]{3,0,2,1:T(8,128)} %copy-done.3, ...), kind=kLoop, calls=%fused_computation.61 | loop fusion | flops 44040192 | bytes 28463376 | tf_op jit(solution)/shard_map/add | solution.py:30
  95.4 5.0 collective-permute-start.7
  100.4 9.5 %collective-permute-done.6 = f32[8,1,16,1024]{3,0,2,1:T(8,128)S(1)} collective-permute-done((f32[8,1,16,1024]{3,0,2,1:T(8,128)S(1)}, f32[8,1,16,1024]{3,0,2,1:T(8,128)S(1)}, u32[]{:S(2)}, u32[]{:S(2)}) %collective-permute-start.6) | collective-permute-done | bytes 524320 | tf_op jit(solution)/shard_map/ppermute | solution.py:20
  112.5 12.8 %collective-permute-start.9 = (f32[8,18,1,1024]{3,0,2,1:T(8,128)S(1)}, f32[8,18,1,1024]{3,0,2,1:T(8,128)S(1)}, u32[]{:S(2)}, u32[]{:S(2)}) collective-permute-start(f32[8,18,1,1024]{3,0,2,1:T(8,128)S(1)} %get-tuple-element.22), channel_id=1, source_target_pairs={{0,2},{2,4},{4,6},{1,3},{3,5},{5,7},{8,10},{10,12},{12,14},{9,11},... | collective-permute-start | bytes 1769480 | tf_op jit(solution)/shard_map/ppermute | solution.py:17
  125.3 12.2 %collective-permute-done.8 = f32[8,18,1,1024]{3,0,2,1:T(8,128)S(1)} collective-permute-done((f32[8,18,1,1024]{3,0,2,1:T(8,128)S(1)}, f32[8,18,1,1024]{3,0,2,1:T(8,128)S(1)}, u32[]{:S(2)}, u32[]{:S(2)}) %collective-permute-start.8) | collective-permute-done | bytes 589856 | tf_op jit(solution)/shard_map/ppermute | solution.py:20
  142.4 3.4 collective-permute-start.11
  147.8 27.8 %fusion.14 = f32[8,16,16,1024]{3,0,2,1:T(8,128)S(1)} fusion(f32[8,18,18,1]{3,0,2,1:T(8,128)S(1)} %copy.70, f32[8,18,1,1024]{3,0,2,1:T(8,128)} %copy-done.8, f32[8,18,1,1024]{3,0,2,1:T(8,128)} %copy-done.10, f32[8,1,16,1024]{3,0,2,1:T(8,128)S(1)} %collective-permute-done.6, f32[8,16,16,1024]{3,0,2,1:T(8,128)} %copy-done, f32[8,1,16,1024]{3,0,2,1:T(8,128)} %copy-done.6, ...), kind=kLoop, calls=%fused_computation.33 | loop fusion | flops 60817408 | bytes 19026192 | tf_op jit(solution)/shard_map/add | solution.py:30
  177.0 5.0 collective-permute-start.13
  182.1 10.0 %collective-permute-done.12 = f32[8,1,16,1024]{3,0,2,1:T(8,128)S(1)} collective-permute-done((f32[8,1,16,1024]{3,0,2,1:T(8,128)S(1)}, f32[8,1,16,1024]{3,0,2,1:T(8,128)S(1)}, u32[]{:S(2)}, u32[]{:S(2)}) %collective-permute-start.12) | collective-permute-done | bytes 524320 | tf_op jit(solution)/shard_map/ppermute | solution.py:20
  194.6 11.8 %collective-permute-start.15 = (f32[8,18,1,1024]{3,0,2,1:T(8,128)S(1)}, f32[8,18,1,1024]{3,0,2,1:T(8,128)S(1)}, u32[]{:S(2)}, u32[]{:S(2)}) collective-permute-start(f32[8,18,1,1024]{3,0,2,1:T(8,128)S(1)} %get-tuple-element.20), channel_id=1, source_target_pairs={{0,2},{2,4},{4,6},{1,3},{3,5},{5,7},{8,10},{10,12},{12,14},{9,11},... | collective-permute-start | bytes 1769480 | tf_op jit(solution)/shard_map/ppermute | solution.py:17
  206.4 12.2 %collective-permute-done.14 = f32[8,18,1,1024]{3,0,2,1:T(8,128)S(1)} collective-permute-done((f32[8,18,1,1024]{3,0,2,1:T(8,128)S(1)}, f32[8,18,1,1024]{3,0,2,1:T(8,128)S(1)}, u32[]{:S(2)}, u32[]{:S(2)}) %collective-permute-start.14) | collective-permute-done | bytes 589856 | tf_op jit(solution)/shard_map/ppermute | solution.py:20
  223.5 3.0 collective-permute-start.17
  228.5 29.4 %fusion.4 = f32[8,16,16,1024]{3,0,2,1:T(8,128)} fusion(f32[8,18,18,1]{3,0,2,1:T(8,128)S(1)} %copy.74, f32[8,18,1,1024]{3,0,2,1:T(8,128)} %copy-done.7, f32[8,18,1,1024]{3,0,2,1:T(8,128)} %copy-done.9, f32[8,1,16,1024]{3,0,2,1:T(8,128)S(1)} %collective-permute-done.12, f32[8,16,16,1024]{3,0,2,1:T(8,128)} %copy-done.1, f32[8,1,16,1024]{3,0,2,1:T(8,128)} %copy-done.5, ...), kind=kLoop, calls=%fused_computation.5 | loop fusion | flops 60817408 | bytes 19026192 | tf_op jit(solution)/shard_map/add | solution.py:30
  257.8 65.8 %copy.78 = f32[8,16,16,1024]{0,3,2,1:T(8,128)} copy(f32[8,16,16,1024]{3,0,2,1:T(8,128)} %fusion.4) | data formatting | bytes 16777216 | tf_op jit(solution)/shard_map/add | solution.py:30
  323.7 21.9 %convolution_bitcast_fusion = f32[8,8]{0,1:T(8,128)S(1)} fusion(f32[8,16,16,1024]{3,0,2,1:T(8,128)} %fusion.4), kind=kOutput, calls=%fused_computation.89 | convolution fusion | flops 201326592 | bytes 8388864 | tf_op jit(solution)/shard_map/dot_general | solution.py:53
  345.6 183.4 %reduce_sum.9 = f32[8,8,8,512]{0,3,2,1:T(8,128)} reduce(f32[8,8,2,8,2,512,2]{0,6,5,4,3,2,1:T(2,128)} %bitcast.9, f32[]{:T(128)} %constant.45.clone.1), dimensions={2,4,6}, to_apply=%region_3.6 | reduce | flops 1835008 | bytes 9437188 | tf_op jit(solution)/shard_map/reduce_sum | solution.py:54
  529.0 9.8 %copy.79 = f32[8,8,8,512]{3,2,1,0:T(8,128)S(1)} copy(f32[8,8,8,512]{0,3,2,1:T(8,128)} %reduce_sum.9) | data formatting | bytes 2097152 | tf_op jit(solution)/shard_map/reduce_sum | solution.py:54
  538.9 2.5 convolution_bitcast_fusion.2
  541.5 52.4 %all-reduce = (f32[8,8]{0,1:T(8,128)S(1)}, f32[8,8]{0,1:T(8,128)S(1)}) all-reduce(f32[8,8]{0,1:T(8,128)S(1)} %convolution_bitcast_fusion, f32[8,8]{0,1:T(8,128)S(1)} %convolution_bitcast_fusion.2), channel_id=1, replica_groups=mesh['gx'=4,'gy'=4,'gz'=2] {'gx','gy','gz'}, use_global_device_ids=true, to_apply=%region_0.0 | all-reduce | flops 128 | bytes 1024 | tf_op jit(solution)/shard_map/psum | solution.py:59
  596.8 1.5 fusion.30
  598.3 1.6 copy.87
  602.8 11.5 %fusion.46 = f32[8,16,16,1024]{3,0,2,1:T(8,128)S(1)} fusion(f32[8,8,1,1]{1,0,3,2:T(8,128)S(1)} %convolution_bitcast_fusion.3, f32[8,16,16,1024]{3,0,2,1:T(8,128)} %fusion.4), kind=kOutput, calls=%fused_computation.132 | convolution fusion | flops 201326592 | bytes 16777472 | tf_op jit(solution)/shard_map/kl,lxyz->kxyz/dot_general | solution.py:42
  614.3 8.3 %copy.86 = f32[8,16,16,1024]{3,2,1,0:T(8,128)} copy(f32[8,16,16,1024]{3,0,2,1:T(8,128)S(1)} %fusion.46) | data formatting | bytes 16777216
  (92 shorter events, 35.3 us)
Async XLA Ops:
  0.6 27.2 %copy-start.4 = (f32[8,16,16,1024]{3,2,1,0:T(8,128)S(1)}, f32[8,16,16,1024]{3,2,1,0:T(8,128)}, u32[]{:S(2)}) copy-start(f32[8,16,16,1024]{3,2,1,0:T(8,128)} %param.5) | copy-start | bytes 25165828
  10.7 6.6 %copy-start.3 = (f32[8,16,16,1024]{3,0,2,1:T(8,128)}, f32[8,16,16,1024]{3,0,2,1:T(8,128)S(1)}, u32[]{:S(2)}) copy-start(f32[8,16,16,1024]{3,0,2,1:T(8,128)S(1)} %copy.57) | copy-start | bytes 25165828
  10.8 16.1 %collective-permute-start.1 = (f32[8,1,16,1024]{3,0,2,1:T(8,128)S(1)}, f32[8,1,16,1024]{3,0,2,1:T(8,128)S(1)}, u32[]{:S(2)}, u32[]{:S(2)}) collective-permute-start(f32[8,1,16,1024]{3,0,2,1:T(8,128)S(1)} %get-tuple-element.31), channel_id=1, source_target_pairs={{0,8},{8,16},{16,24},{1,9},{9,17},{17,25},{2,10},{10,18},{18,26},{... | collective-permute-start | bytes 1572872 | tf_op jit(solution)/shard_map/ppermute | solution.py:17
  15.8 19.1 %collective-permute-start = (f32[8,1,16,1024]{3,0,2,1:T(8,128)S(1)}, f32[8,1,16,1024]{3,0,2,1:T(8,128)S(1)}, u32[]{:S(2)}, u32[]{:S(2)}) collective-permute-start(f32[8,1,16,1024]{3,0,2,1:T(8,128)S(1)} %get-tuple-element.30), channel_id=1, source_target_pairs={{8,0},{16,8},{24,16},{9,1},{17,9},{25,17},{10,2},{18,10},{26,18},{... | collective-permute-start | bytes 1572872 | tf_op jit(solution)/shard_map/ppermute | solution.py:20
  27.8 13.3 %copy-start.14 = (s32[3,2]{0,1:T(2,128)S(1)}, s32[3,2]{0,1:T(2,128)}, u32[]{:S(2)}) copy-start(s32[3,2]{0,1:T(2,128)} %param.6) | copy-start | bytes 76
  35.0 18.8 %copy-start.13 = (f32[8,1,16,1024]{3,0,2,1:T(8,128)}, f32[8,1,16,1024]{3,0,2,1:T(8,128)S(1)}, u32[]{:S(2)}) copy-start(f32[8,1,16,1024]{3,0,2,1:T(8,128)S(1)} %collective-permute-done) | copy-start | bytes 1572868
  35.0 18.2 %copy-start.2 = (f32[8,18,16,1024]{3,0,2,1:T(8,128)}, f32[8,18,16,1024]{3,0,2,1:T(8,128)S(1)}, u32[]{:S(2)}) copy-start(f32[8,18,16,1024]{3,0,2,1:T(8,128)S(1)} %constant_dynamic-update-slice_fusion) | copy-start | bytes 28311556
  35.2 18.1 %collective-permute-start.2 = (f32[8,18,1,1024]{3,0,2,1:T(8,128)S(1)}, f32[8,18,1,1024]{3,0,2,1:T(8,128)S(1)}, u32[]{:S(2)}, u32[]{:S(2)}) collective-permute-start(f32[8,18,1,1024]{3,0,2,1:T(8,128)S(1)} %get-tuple-element.25), channel_id=1, source_target_pairs={{2,0},{4,2},{6,4},{3,1},{5,3},{7,5},{10,8},{12,10},{14,12},{11,9},... | collective-permute-start | bytes 1769480 | tf_op jit(solution)/shard_map/ppermute | solution.py:20
  36.5 16.8 %collective-permute-start.3 = (f32[8,18,1,1024]{3,0,2,1:T(8,128)S(1)}, f32[8,18,1,1024]{3,0,2,1:T(8,128)S(1)}, u32[]{:S(2)}, u32[]{:S(2)}) collective-permute-start(f32[8,18,1,1024]{3,0,2,1:T(8,128)S(1)} %get-tuple-element.24), channel_id=1, source_target_pairs={{0,2},{2,4},{4,6},{1,3},{3,5},{5,7},{8,10},{10,12},{12,14},{9,11},... | collective-permute-start | bytes 1769480 | tf_op jit(solution)/shard_map/ppermute | solution.py:17
  53.3 0.8 copy-start.11
  55.0 7.9 %collective-permute-start.4 = (f32[8,18,18,1]{2,0,3,1:T(8,128)S(1)}, f32[8,18,18,1]{2,0,3,1:T(8,128)S(1)}, u32[]{:S(2)}, u32[]{:S(2)}) collective-permute-start(f32[8,18,18,1]{2,0,3,1:T(8,128)S(1)} %copy.63), channel_id=1, source_target_pairs={{1,0},{3,2},{5,4},{7,6},{9,8},{11,10},{13,12},{15,14},{17,16},{19,... | collective-permute-start | bytes 31112 | tf_op jit(solution)/shard_map/ppermute | solution.py:20
  57.3 6.7 %collective-permute-start.5 = (f32[8,18,18,1]{2,0,3,1:T(8,128)S(1)}, f32[8,18,18,1]{2,0,3,1:T(8,128)S(1)}, u32[]{:S(2)}, u32[]{:S(2)}) collective-permute-start(f32[8,18,18,1]{2,0,3,1:T(8,128)S(1)} %copy.65), channel_id=1, source_target_pairs={{0,1},{2,3},{4,5},{6,7},{8,9},{10,11},{12,13},{14,15},{16,17},{18,... | collective-permute-start | bytes 31112 | tf_op jit(solution)/shard_map/ppermute | solution.py:17
  93.9 44.9 %copy-start = (f32[8,16,16,1024]{3,0,2,1:T(8,128)}, f32[8,16,16,1024]{3,0,2,1:T(8,128)S(1)}, u32[]{:S(2)}) copy-start(f32[8,16,16,1024]{3,0,2,1:T(8,128)S(1)} %fusion.24) | copy-start | bytes 25165828
  94.1 15.9 %collective-permute-start.6 = (f32[8,1,16,1024]{3,0,2,1:T(8,128)S(1)}, f32[8,1,16,1024]{3,0,2,1:T(8,128)S(1)}, u32[]{:S(2)}, u32[]{:S(2)}) collective-permute-start(f32[8,1,16,1024]{3,0,2,1:T(8,128)S(1)} %get-tuple-element.29), channel_id=1, source_target_pairs={{8,0},{16,8},{24,16},{9,1},{17,9},{25,17},{10,2},{18,10},{26,18},{... | collective-permute-start | bytes 1572872 | tf_op jit(solution)/shard_map/ppermute | solution.py:20
  95.4 15.7 %collective-permute-start.7 = (f32[8,1,16,1024]{3,0,2,1:T(8,128)S(1)}, f32[8,1,16,1024]{3,0,2,1:T(8,128)S(1)}, u32[]{:S(2)}, u32[]{:S(2)}) collective-permute-start(f32[8,1,16,1024]{3,0,2,1:T(8,128)S(1)} %get-tuple-element.28), channel_id=1, source_target_pairs={{0,8},{8,16},{16,24},{1,9},{9,17},{17,25},{2,10},{10,18},{18,26},{... | collective-permute-start | bytes 1572872 | tf_op jit(solution)/shard_map/ppermute | solution.py:17
  111.1 27.7 %copy-start.6 = (f32[8,1,16,1024]{3,0,2,1:T(8,128)}, f32[8,1,16,1024]{3,0,2,1:T(8,128)S(1)}, u32[]{:S(2)}) copy-start(f32[8,1,16,1024]{3,0,2,1:T(8,128)S(1)} %collective-permute-done.7) | copy-start | bytes 1572868
  111.2 26.3 %collective-permute-start.8 = (f32[8,18,1,1024]{3,0,2,1:T(8,128)S(1)}, f32[8,18,1,1024]{3,0,2,1:T(8,128)S(1)}, u32[]{:S(2)}, u32[]{:S(2)}) collective-permute-start(f32[8,18,1,1024]{3,0,2,1:T(8,128)S(1)} %get-tuple-element.23), channel_id=1, source_target_pairs={{2,0},{4,2},{6,4},{3,1},{5,3},{7,5},{10,8},{12,10},{14,12},{11,9},... | collective-permute-start | bytes 1769480 | tf_op jit(solution)/shard_map/ppermute | solution.py:20
  112.5 25.0 %collective-permute-start.9 = (f32[8,18,1,1024]{3,0,2,1:T(8,128)S(1)}, f32[8,18,1,1024]{3,0,2,1:T(8,128)S(1)}, u32[]{:S(2)}, u32[]{:S(2)}) collective-permute-start(f32[8,18,1,1024]{3,0,2,1:T(8,128)S(1)} %get-tuple-element.22), channel_id=1, source_target_pairs={{0,2},{2,4},{4,6},{1,3},{3,5},{5,7},{8,10},{10,12},{12,14},{9,11},... | collective-permute-start | bytes 1769480 | tf_op jit(solution)/shard_map/ppermute | solution.py:17
  137.5 0.8 copy-start.8
  138.3 0.9 copy-start.10
  140.1 5.7 collective-permute-start.10
  142.4 4.4 collective-permute-start.11
  175.6 44.3 %copy-start.1 = (f32[8,16,16,1024]{3,0,2,1:T(8,128)}, f32[8,16,16,1024]{3,0,2,1:T(8,128)S(1)}, u32[]{:S(2)}) copy-start(f32[8,16,16,1024]{3,0,2,1:T(8,128)S(1)} %fusion.14) | copy-start | bytes 25165828
  175.7 16.3 %collective-permute-start.12 = (f32[8,1,16,1024]{3,0,2,1:T(8,128)S(1)}, f32[8,1,16,1024]{3,0,2,1:T(8,128)S(1)}, u32[]{:S(2)}, u32[]{:S(2)}) collective-permute-start(f32[8,1,16,1024]{3,0,2,1:T(8,128)S(1)} %get-tuple-element.27), channel_id=1, source_target_pairs={{8,0},{16,8},{24,16},{9,1},{17,9},{25,17},{10,2},{18,10},{26,18},{... | collective-permute-start | bytes 1572872 | tf_op jit(solution)/shard_map/ppermute | solution.py:20
  177.0 16.2 %collective-permute-start.13 = (f32[8,1,16,1024]{3,0,2,1:T(8,128)S(1)}, f32[8,1,16,1024]{3,0,2,1:T(8,128)S(1)}, u32[]{:S(2)}, u32[]{:S(2)}) collective-permute-start(f32[8,1,16,1024]{3,0,2,1:T(8,128)S(1)} %get-tuple-element.26), channel_id=1, source_target_pairs={{0,8},{8,16},{16,24},{1,9},{9,17},{17,25},{2,10},{10,18},{18,26},{... | collective-permute-start | bytes 1572872 | tf_op jit(solution)/shard_map/ppermute | solution.py:17
  193.2 26.7 %copy-start.5 = (f32[8,1,16,1024]{3,0,2,1:T(8,128)}, f32[8,1,16,1024]{3,0,2,1:T(8,128)S(1)}, u32[]{:S(2)}) copy-start(f32[8,1,16,1024]{3,0,2,1:T(8,128)S(1)} %collective-permute-done.13) | copy-start | bytes 1572868
  193.3 25.3 %collective-permute-start.14 = (f32[8,18,1,1024]{3,0,2,1:T(8,128)S(1)}, f32[8,18,1,1024]{3,0,2,1:T(8,128)S(1)}, u32[]{:S(2)}, u32[]{:S(2)}) collective-permute-start(f32[8,18,1,1024]{3,0,2,1:T(8,128)S(1)} %get-tuple-element.21), channel_id=1, source_target_pairs={{2,0},{4,2},{6,4},{3,1},{5,3},{7,5},{10,8},{12,10},{14,12},{11,9},... | collective-permute-start | bytes 1769480 | tf_op jit(solution)/shard_map/ppermute | solution.py:20
  194.6 24.0 %collective-permute-start.15 = (f32[8,18,1,1024]{3,0,2,1:T(8,128)S(1)}, f32[8,18,1,1024]{3,0,2,1:T(8,128)S(1)}, u32[]{:S(2)}, u32[]{:S(2)}) collective-permute-start(f32[8,18,1,1024]{3,0,2,1:T(8,128)S(1)} %get-tuple-element.20), channel_id=1, source_target_pairs={{0,2},{2,4},{4,6},{1,3},{3,5},{5,7},{8,10},{10,12},{12,14},{9,11},... | collective-permute-start | bytes 1769480 | tf_op jit(solution)/shard_map/ppermute | solution.py:17
  218.6 0.8 copy-start.7
  219.4 0.9 copy-start.9
  221.2 5.3 collective-permute-start.16
  223.5 4.0 collective-permute-start.17
  (1 other events, 0.8 us)
where the time goes:
time: 631 us; the launch traced here: 623 us
  other arithmetic  277 us (44%)
  local copies, waits for them, and re-layouts  119 us (19%)
  waiting for transfers between devices  68.1 us (11%)
  starting transfers between devices  65.7 us (10%)
  blocking collectives  52.4 us (8%)
  matrix products  37.8 us (6%)
    reduce_sum x1, other arithmetic, local(): fields.reshape(vectors, rows_x // 2, 2, rows_y // 2, 2, rows_z // 2, 2)  183 us
    add x3, other arithmetic, jacobi_sweep(): return (1.0 - omega_weight) * center + scaled * beside  86.1 us
    add x1, local copies, waits for them, and re-layouts, jacobi_sweep(): return (1.0 - omega_weight) * center + scaled * beside  65.8 us
    ppermute x9, waiting for transfers between devices, extended(): lax.ppermute(lax.slice_in_dim(block, 0, width, axis=dim), axis, backward)  56 us
    ppermute x9, starting transfers between devices, extended(): lax.ppermute(lax.slice_in_dim(block, block.shape[dim] - width, None, axis...  53.9 us
    psum x1, blocking collectives, local(): lax.psum((gram_part, coarse_part), ('gx', 'gy', 'gz'))  52.4 us
    unnamed x35, local copies, waits for them, and re-layouts  30.5 us
    dot_general x1, matrix products, local(): gram_part = jnp.dot(flattened, flattened.T, precision=lax.Precision.HIGHEST)  21.9 us
  transfers between devices with their start and end apart: 18, of which 8 were waited for; matrix products, arithmetic and copies ran while one was open for 2% of the time, Pallas kernels for 0%

commit v1 on v0

v1 whole, which is shorter than its diff:
```python
import functools

import jax
import jax.numpy as jnp
from jax import lax
from jax.experimental import pallas as pl
from jax.experimental.pallas import tpu as pltpu
from jax.sharding import PartitionSpec as P

SWEEPS = 3
OMEGA = 2.0 / 3.0
MESH = pl.DeviceIdType.MESH
HIGHEST = lax.Precision.HIGHEST
AXES = ("gx", "gy", "gz")


def inverse_factor(gram):
    k = gram.shape[0]
    row = lax.broadcasted_iota(jnp.int32, gram.shape, 0)
    lane = lax.broadcasted_iota(jnp.int32, gram.shape, 1)
    m = jnp.where(lane < k, gram, 0.0) + jnp.where(lane == row + k, 1.0, 0.0)
    scale = jnp.zeros(gram.shape, jnp.float32)
    for j in range(k):
        pivot_row = m[j : j + 1, :]
        pivot = pivot_row[:, j : j + 1]
        column = m[:, j : j + 1]
        scale = jnp.where(row == j, pivot, scale)
        m = m - jnp.where(row > j, (column / pivot) * pivot_row, 0.0)
    return m / jnp.sqrt(scale)


def relax_kernel(
    sizes, cells, aniso_ref, v_ref, f_out, c_out, inv_ref, cinv_ref,
    f0, f1, f2, ys, yh, zh, cs, gp, cgp, *rest,
):
    gbs, (in_sem, out_sem, c_sem, send_sem, recv_sem, gsend, grecv) = rest[:3], rest[3:]
    vectors, rows_x, rows_y, rows_z = v_ref.shape
    me = {axis: lax.axis_index(axis) for axis in AXES}
    bufs = (f0, f1, f2)

    def load(k):
        return pltpu.make_async_copy(v_ref.at[k], f0.at[k, pl.ds(1, rows_x)], in_sem.at[k])

    for k in range(vectors):
        load(k).start()

    def halo(r, k, axis, side):
        f = bufs[r]
        if axis == 0:
            src = f.at[k, rows_x if side == 0 else 1]
            dst = f.at[k, 0 if side == 0 else rows_x + 1]
        elif axis == 1:
            src = ys.at[r, side, k]
            dst = yh.at[r, side, k]
        else:
            src = f.at[k, pl.ds(1, rows_x), :, pl.ds(rows_z - 128 if side == 0 else 0, 128)]
            dst = zh.at[r, side, k]
        name = AXES[axis]
        target = me[name] + 1 if side == 0 else me[name] - 1
        return pltpu.make_async_remote_copy(
            src_ref=src,
            dst_ref=dst,
            send_sem=send_sem.at[r, k, axis, side],
            recv_sem=recv_sem.at[r, k, axis, side],
            device_id={name: target},
            device_id_type=MESH,
        )

    def sends_to(axis, side):
        name = AXES[axis]
        return me[name] < sizes[axis] - 1 if side == 0 else me[name] > 0

    def gets_from(axis, side):
        name = AXES[axis]
        return me[name] > 0 if side == 0 else me[name] < sizes[axis] - 1

    barrier = pltpu.get_barrier_semaphore()
    peers = 0
    for axis, name in enumerate(AXES):
        for d in range(1, sizes[axis]):
            pl.semaphore_signal(
                barrier, inc=1,
                device_id={name: lax.rem(me[name] + d, sizes[axis])}, device_id_type=MESH,
            )
            peers += 1

    for axis in range(2):
        for side in range(2):
            @pl.when(jnp.logical_not(gets_from(axis, side)))
            def _():
                def clear(k, _):
                    for r in range(SWEEPS):
                        zero = jnp.zeros((rows_y if axis == 0 else rows_x, rows_z), jnp.float32)
                        if axis == 0:
                            bufs[r][k, 0 if side == 0 else rows_x + 1] = zero
                        else:
                            yh[r, side, k] = zero
                    return 0

                lax.fori_loop(0, vectors, clear, 0)

    def quotient(d):
        top = jnp.full((8, 128), aniso_ref[d, 0], jnp.int32).astype(jnp.float32)
        return top / jnp.full((8, 128), aniso_ref[d, 1], jnp.int32).astype(jnp.float32)

    coefficients = [quotient(d) for d in range(3)]
    scaled = OMEGA / (2.0 * (coefficients[0] + coefficients[1] + coefficients[2]))
    reps = (rows_y // 8, rows_z // 128)
    w = [jnp.tile(c * scaled, reps) for c in coefficients]

    pl.semaphore_wait(barrier, peers)

    def pack(r, k):
        f = bufs[r]
        for x in range(rows_x):
            ys[r, 0, k, pl.ds(x, 1), :] = f[k, x + 1, pl.ds(rows_y - 1, 1), :]
            ys[r, 1, k, pl.ds(x, 1), :] = f[k, x + 1, pl.ds(0, 1), :]

    def send(r, k):
        for axis in range(3):
            for side in range(2):
                @pl.when(sends_to(axis, side))
                def _():
                    halo(r, k, axis, side).start()

    def receive(r, k):
        for axis in range(3):
            for side in range(2):
                @pl.when(gets_from(axis, side))
                def _():
                    halo(r, k, axis, side).wait_recv()

    def finish_send(r, k):
        for axis in range(3):
            for side in range(2):
                @pl.when(sends_to(axis, side))
                def _():
                    halo(r, k, axis, side).wait_send()

    def first(k, _):
        load(k).wait()
        pack(0, k)
        send(0, k)
        return 0

    lax.fori_loop(0, vectors, first, 0)

    lane = lax.broadcasted_iota(jnp.int32, (rows_y, 128), 1)
    row = lax.broadcasted_iota(jnp.int32, (rows_y, rows_z), 0)
    use_high = jnp.logical_and(lane < 64, gets_from(2, 1))
    use_low = jnp.logical_and(lane >= 64, gets_from(2, 0))

    def sweep(r, k):
        f, out = bufs[r], bufs[(r + 1) % 3]

        def body(x, _):
            c = f[k, x + 1]
            side_z = jnp.where(use_high, zh[r, 1, k, x], jnp.where(use_low, zh[r, 0, k, x], 0.0))
            wide = jnp.concatenate([c, side_z], axis=1)
            width = rows_z + 128
            beside_z = pltpu.roll(wide, 1, 1)[:, :rows_z] + pltpu.roll(wide, width - 1, 1)[:, :rows_z]
            below = jnp.where(row == 0, yh[r, 0, k, pl.ds(x, 1), :], pltpu.roll(c, 1, 0))
            above = jnp.where(
                row == rows_y - 1, yh[r, 1, k, pl.ds(x, 1), :], pltpu.roll(c, rows_y - 1, 0)
            )
            total = w[0] * (f[k, x] + f[k, x + 2]) + w[1] * (below + above) + w[2] * beside_z
            out[k, x + 1] = (1.0 - OMEGA) * c + total
            return 0

        lax.fori_loop(0, rows_x, body, 0)

    for r in range(SWEEPS - 1):
        def step(k, _):
            receive(r, k)
            sweep(r, k)
            pack(r + 1, k)
            send(r + 1, k)
            return 0

        lax.fori_loop(0, vectors, step, 0)

    pair_z = jnp.where(
        lax.broadcasted_iota(jnp.int32, (256, 128), 0) // 2
        == lax.broadcasted_iota(jnp.int32, (256, 128), 1),
        0.125, 0.0,
    )
    half = rows_x // 2 * rows_y
    pair_y = jnp.where(
        lax.broadcasted_iota(jnp.int32, (half // 2, half), 0)
        == lax.broadcasted_iota(jnp.int32, (half // 2, half), 1) // 2,
        1.0, 0.0,
    )

    def tile_sum(product):
        parts = [
            product[i : i + 8, j : j + 128]
            for i in range(0, product.shape[0], 8)
            for j in range(0, product.shape[1], 128)
        ]
        while len(parts) > 1:
            parts = [sum(parts[i : i + 2]) for i in range(0, len(parts), 2)]
        return parts[0]

    def out_copy(k):
        return pltpu.make_async_copy(f0.at[k, pl.ds(1, rows_x)], f_out.at[k], out_sem.at[k])

    def coarse_copy(k):
        return pltpu.make_async_copy(cs.at[k], c_out.at[k], c_sem.at[k])

    def last(k, _):
        receive(SWEEPS - 1, k)
        finish_send(0, k)
        sweep(SWEEPS - 1, k)
        out_copy(k).start()
        for j in range(rows_z // 256):
            block = jnp.concatenate(
                [
                    f0[k, 2 * x + 1, :, pl.ds(256 * j, 256)] + f0[k, 2 * x + 2, :, pl.ds(256 * j, 256)]
                    for x in range(rows_x // 2)
                ],
                axis=0,
            )
            thin = jnp.dot(block, pair_z, precision=HIGHEST, preferred_element_type=jnp.float32)
            mean = jnp.dot(pair_y, thin, precision=HIGHEST, preferred_element_type=jnp.float32)
            cs[k, :, :, pl.ds(128 * j, 128)] = mean.reshape(rows_x // 2, rows_y // 2, 128)
        coarse_copy(k).start()

        def pair(l, _):
            def add(x, acc):
                return acc + tile_sum(f0[k, x + 1] * f0[l, x + 1])

            acc = lax.fori_loop(0, rows_x, add, jnp.zeros((8, 128), jnp.float32))
            line = jnp.sum(acc, axis=0, keepdims=True)
            gp[l, pl.ds(k, 1), :] = line
            gp[k, pl.ds(l, 1), :] = line
            acc = jnp.zeros((8, 128), jnp.float32)
            for x in range(rows_x // 2):
                acc = acc + tile_sum(cs[k, x] * cs[l, x])
            line = jnp.sum(acc, axis=0, keepdims=True)
            cgp[l, pl.ds(k, 1), :] = line
            cgp[k, pl.ds(l, 1), :] = line
            return 0

        lax.fori_loop(0, k + 1, pair, 0)
        return 0

    lax.fori_loop(0, vectors, last, 0)

    lane8 = lax.broadcasted_iota(jnp.int32, (vectors, 128), 1)
    gram = jnp.zeros((vectors, 128), jnp.float32)
    for l in range(vectors):
        gram = jnp.where(lane8 == l, jnp.sum(gp[l], axis=1, keepdims=True), gram)
        gram = jnp.where(lane8 == l + 64, jnp.sum(cgp[l], axis=1, keepdims=True), gram)

    for axis, name in enumerate(AXES):
        gb = gbs[axis]
        here = me[name]
        gb[here] = gram
        copies = [
            pltpu.make_async_remote_copy(
                src_ref=gb.at[here],
                dst_ref=gb.at[here],
                send_sem=gsend.at[axis, d],
                recv_sem=grecv.at[axis, d],
                device_id={name: lax.rem(here + d, sizes[axis])},
                device_id_type=MESH,
            )
            for d in range(1, sizes[axis])
        ]
        for copy in copies:
            copy.start()
        for d in range(1, sizes[axis]):
            source = lax.rem(here + sizes[axis] - d, sizes[axis])
            pltpu.make_async_remote_copy(
                src_ref=gb.at[source],
                dst_ref=gb.at[source],
                send_sem=gsend.at[axis, d],
                recv_sem=grecv.at[axis, d],
                device_id={name: lax.rem(here + d, sizes[axis])},
                device_id_type=MESH,
            ).wait_recv()
        for copy in copies:
            copy.wait_send()
        gram = gb[0]
        for i in range(1, sizes[axis]):
            gram = gram + gb[i]

    inv_ref[...] = inverse_factor(gram / cells)
    cinv_ref[...] = inverse_factor(pltpu.roll(gram, 64, 1) / (cells // 8))

    def drain(k, _):
        for r in range(1, SWEEPS):
            finish_send(r, k)
        out_copy(k).wait()
        coarse_copy(k).wait()
        return 0

    lax.fori_loop(0, vectors, drain, 0)


def apply_kernel(inv_ref, cinv_ref, f_ref, c_ref, b_ref, cb_ref):
    k_count = f_ref.shape[0]

    def combine(factor, src, dst, columns):
        data = [src[l, 0, :, columns] for l in range(k_count)]
        for k in range(k_count):
            total = factor[k, k_count] * data[0]
            for l in range(1, k + 1):
                total = total + factor[k, k_count + l] * data[l]
            dst[k, 0, :, columns] = total

    for j in range(0, f_ref.shape[3], 128):
        combine(inv_ref, f_ref, b_ref, pl.ds(j, 128))
    for j in range(0, c_ref.shape[3], 128):
        combine(cinv_ref, c_ref, cb_ref, pl.ds(j, 128))


def local(sizes, test_vectors, aniso):
    vectors, rows_x, rows_y, rows_z = test_vectors.shape
    coarse_shape = (vectors, rows_x // 2, rows_y // 2, rows_z // 2)
    cells = rows_x * rows_y * rows_z * sizes[0] * sizes[1] * sizes[2]
    f32 = jnp.float32
    field = pltpu.VMEM((vectors, rows_x + 2, rows_y, rows_z), f32)
    most = max(sizes)
    small = jax.ShapeDtypeStruct((vectors, 128), f32)
    fields, coarse, inv, cinv = pl.pallas_call(
        functools.partial(relax_kernel, sizes, cells),
        out_shape=(
            jax.ShapeDtypeStruct(test_vectors.shape, f32),
            jax.ShapeDtypeStruct(coarse_shape, f32),
            small,
            small,
        ),
        in_specs=[pl.BlockSpec(memory_space=pltpu.SMEM), pl.BlockSpec(memory_space=pl.ANY)],
        out_specs=(
            pl.BlockSpec(memory_space=pl.ANY),
            pl.BlockSpec(memory_space=pl.ANY),
            pl.BlockSpec(memory_space=pltpu.VMEM),
            pl.BlockSpec(memory_space=pltpu.VMEM),
        ),
        scratch_shapes=[
            field,
            field,
            field,
            pltpu.VMEM((SWEEPS, 2, vectors, rows_x, rows_z), f32),
            pltpu.VMEM((SWEEPS, 2, vectors, rows_x, rows_z), f32),
            pltpu.VMEM((SWEEPS, 2, vectors, rows_x, rows_y, 128), f32),
            pltpu.VMEM(coarse_shape, f32),
            pltpu.VMEM((vectors, vectors, 128), f32),
            pltpu.VMEM((vectors, vectors, 128), f32),
            *[pltpu.VMEM((n, vectors, 128), f32) for n in sizes],
            pltpu.SemaphoreType.DMA((vectors,)),
            pltpu.SemaphoreType.DMA((vectors,)),
            pltpu.SemaphoreType.DMA((vectors,)),
            pltpu.SemaphoreType.DMA((SWEEPS, vectors, 3, 2)),
            pltpu.SemaphoreType.DMA((SWEEPS, vectors, 3, 2)),
            pltpu.SemaphoreType.DMA((3, most)),
            pltpu.SemaphoreType.DMA((3, most)),
        ],
        compiler_params=pltpu.CompilerParams(
            collective_id=0, has_side_effects=True, vmem_limit_bytes=60 * 2**20
        ),
    )(aniso, test_vectors)
    block = pl.BlockSpec((vectors, 1, rows_y, rows_z), lambda i: (0, i, 0, 0))
    coarse_block = pl.BlockSpec(
        (vectors, 1, rows_y // 2, rows_z // 4), lambda i: (0, i // 2, 0, i % 2)
    )
    factor = pl.BlockSpec(memory_space=pltpu.SMEM)
    return pl.pallas_call(
        apply_kernel,
        grid=(rows_x,),
        out_shape=(
            jax.ShapeDtypeStruct(test_vectors.shape, f32),
            jax.ShapeDtypeStruct(coarse_shape, f32),
        ),
        in_specs=[factor, factor, block, coarse_block],
        out_specs=(block, coarse_block),
    )(inv, cinv, fields, coarse)


def solution(mesh):
    sizes = tuple(mesh.shape[axis] for axis in AXES)
    spec = P(None, *AXES)
    return jax.shard_map(
        functools.partial(local, sizes),
        mesh=mesh,
        in_specs=(spec, P()),
        out_specs=(spec, spec),
        check_vma=False,
    )
```

time: 631 us -> 119 us (0.19); the launches traced: 623 us -> 118 us
  other arithmetic: 277 us -> 0 us
  local copies, waits for them, and re-layouts: 119 us -> 1.34 us
  Pallas kernels: 0 us -> 116 us
  waiting for transfers between devices: 68.1 us -> 0 us
  starting transfers between devices: 65.7 us -> 0 us
  blocking collectives: 52.4 us -> 0 us
  matrix products: 37.8 us -> 0 us
    reduce_sum x1 -> x0, other arithmetic: 183 us -> none  [local(): fields.reshape(vectors, rows_x // 2, 2, rows_y // 2, 2, rows_z // 2, 2)]
    pallas_call x0 -> x2, Pallas kernels: none -> 116 us  [the longest x1 103 us: local(): pl.pallas_call(functools.partial(relax_kernel, sizes, cells), out_shape=(...]
    add x3 -> x0, other arithmetic: 86.1 us -> none  [jacobi_sweep(): return (1.0 - omega_weight) * center + scaled * beside]
    ppermute x18 -> x0, waiting for transfers between devices: 68.1 us -> none  [the longest x9 56 us: extended(): lax.ppermute(lax.slice_in_dim(block, 0, width, axis=dim), axis, backward)]
    add x1 -> x0, local copies, waits for them, and re-layouts: 65.8 us -> none  [jacobi_sweep(): return (1.0 - omega_weight) * center + scaled * beside]
    ppermute x18 -> x0, starting transfers between devices: 65.7 us -> none  [the longest x9 53.9 us: extended(): lax.ppermute(lax.slice_in_dim(block, block.shape[dim] - width, None, axis...]
    psum x1 -> x0, blocking collectives: 52.4 us -> none  [local(): lax.psum((gram_part, coarse_part), ('gx', 'gy', 'gz'))]
    dot_general x4 -> x0, matrix products: 37.5 us -> none  [the longest x1 21.9 us: local(): gram_part = jnp.dot(flattened, flattened.T, precision=lax.Precision.HIGHEST)]
  transfers between devices with their start and end apart: 18 -> 0, of which waited for: 8 -> 0; matrix products, arithmetic and copies ran while one was open for 2% -> 0% of each run, Pallas kernels for 0% -> 0%
where the time goes in v1:
time: 119 us; the launch traced here: 118 us
  Pallas kernels  116 us (97%)
  local copies, waits for them, and re-layouts  1.34 us (1%)
    pallas_call x1, Pallas kernels, local(): pl.pallas_call(functools.partial(relax_kernel, sizes, cells), out_shape=(...  103 us
    pallas_call x1, Pallas kernels, local(): pl.pallas_call(apply_kernel, grid=(rows_x,), out_shape=(jax.ShapeDtypeStr...  13.4 us

profile of v1, /device:TPU:0, one launch (start us, length us, event | category | flops | bytes accessed | tf_op | source)
XLA Modules:
  0.0 118.4 jit_solution(13187655345976153735)
XLA Ops:
  0.6 1.3 %copy.4.aniso_ref = s32[3,2]{1,0:T(4,128)} copy(s32[3,2]{0,1:T(2,128)} %param.3) | data formatting | bytes 48 | tf_op args[1]
  2.0 103.0 %shard_map.41 = (f32[8,16,16,1024]{3,2,1,0:T(8,128)}, f32[8,8,8,512]{3,2,1,0:T(8,128)}, f32[8,128]{1,0:T(8,128)}, f32[8,128]{1,0:T(8,128)}) custom-call(s32[3,2]{1,0:T(4,128)} %copy.4.aniso_ref, f32[8,16,16,1024]{3,2,1,0:T(8,128)} %v_ref.1), custom_call_target="tpu_custom_call" | custom-call | tf_op jit(solution)/shard_map/pallas_call | solution.py:326
  105.0 13.4 %shard_map.42 = (f32[8,16,16,1024]{3,2,1,0:T(8,128)}, f32[8,8,8,512]{3,2,1,0:T(8,128)}) custom-call(f32[8,128]{1,0:T(8,128)} %get-tuple-element.6.inv_ref, f32[8,128]{1,0:T(8,128)} %get-tuple-element.7.cinv_ref, f32[8,16,16,1024]{3,2,1,0:T(8,128)} %get-tuple-element.8.f_ref, f32[8,8,8,512]{3,2,1,0:T(8,128)} %get-tuple-element.9.c_ref), custom_call_target="tpu_custom_call" | custom-call | tf_op jit(solution)/shard_map/pallas_call | solution.py:369

commit v2 on v1

--- a/solution.py
+++ b/solution.py
@@ -8,6 +8,7 @@
 from jax.sharding import PartitionSpec as P
 
 SWEEPS = 3
+SWEEP_UNROLL = 16
 OMEGA = 2.0 / 3.0
 MESH = pl.DeviceIdType.MESH
 HIGHEST = lax.Precision.HIGHEST
@@ -30,10 +31,11 @@
 
 
 def relax_kernel(
-    sizes, cells, aniso_ref, v_ref, f_out, c_out, inv_ref, cinv_ref,
-    f0, f1, f2, ys, yh, zh, cs, gp, cgp, *rest,
+    sizes, cells, relayed, aniso_ref, v_ref, f_out, c_out, inv_ref, cinv_ref,
+    f0, f1, f2, ys, yh, zh, rb, thin, cs, gp, cgp, gb, *rest,
 ):
-    gbs, (in_sem, out_sem, c_sem, send_sem, recv_sem, gsend, grecv) = rest[:3], rest[3:]
+    in_sem, out_sem, c_sem, send_sem, recv_sem, gsend, grecv, *relay_sems = rest
+    up_send, up_recv, down_send, down_recv = relay_sems
     vectors, rows_x, rows_y, rows_z = v_ref.shape
     me = {axis: lax.axis_index(axis) for axis in AXES}
     bufs = (f0, f1, f2)
@@ -66,23 +68,72 @@
             device_id_type=MESH,
         )
 
-    def sends_to(axis, side):
-        name = AXES[axis]
-        return me[name] < sizes[axis] - 1 if side == 0 else me[name] > 0
-
     def gets_from(axis, side):
         name = AXES[axis]
         return me[name] > 0 if side == 0 else me[name] < sizes[axis] - 1
 
+    def direct_to(axis, side):
+        name = AXES[axis]
+        there = me[name] < sizes[axis] - 1 if side == 0 else me[name] > 0
+        if relayed and axis == 1:
+            there = jnp.logical_and(there, me[name] != (1 if side == 0 else 2))
+        return there
+
+    def direct_from(axis, side):
+        there = gets_from(axis, side)
+        if relayed and axis == 1:
+            there = jnp.logical_and(there, me["gy"] != (2 if side == 0 else 1))
+        return there
+
+    part = rows_x // 2
+    ways = ((0, 1, 2), (1, 2, 1))
+    relays = ((0, 0), (1, 3))
+
+    def to_relay(r, k, side, half, by):
+        return pltpu.make_async_remote_copy(
+            src_ref=ys.at[r, side, k, pl.ds(half * part, part)],
+            dst_ref=rb.at[r, side, k],
+            send_sem=up_send.at[r, k, half],
+            recv_sem=up_recv.at[r, k, side],
+            device_id={"gy": by},
+            device_id_type=MESH,
+        )
+
+    def from_relay(r, k, side, half, target):
+        return pltpu.make_async_remote_copy(
+            src_ref=rb.at[r, side, k],
+            dst_ref=yh.at[r, side, k, pl.ds(half * part, part)],
+            send_sem=down_send.at[r, k, side],
+            recv_sem=down_recv.at[r, k, half],
+            device_id={"gy": target},
+            device_id_type=MESH,
+        )
+
+    def forward(r, k):
+        for half, by in relays if relayed else ():
+            @pl.when(me["gy"] == by)
+            def _():
+                for side, source, target in ways:
+                    to_relay(r, k, side, half, by).wait_recv()
+                    from_relay(r, k, side, half, target).start()
+
     barrier = pltpu.get_barrier_semaphore()
-    peers = 0
-    for axis, name in enumerate(AXES):
-        for d in range(1, sizes[axis]):
-            pl.semaphore_signal(
-                barrier, inc=1,
-                device_id={name: lax.rem(me[name] + d, sizes[axis])}, device_id_type=MESH,
-            )
-            peers += 1
+    devices = sizes[0] * sizes[1] * sizes[2]
+    here = (me["gx"] * sizes[1] + me["gy"]) * sizes[2] + me["gz"]
+
+    def place(index):
+        return {
+            "gx": index // (sizes[1] * sizes[2]),
+            "gy": lax.rem(index // sizes[2], sizes[1]),
+            "gz": lax.rem(index, sizes[2]),
+        }
+
+    def greet(d, _):
+        other = place(lax.rem(here + d, devices))
+        pl.semaphore_signal(barrier, inc=1, device_id=other, device_id_type=MESH)
+        return 0
+
+    lax.fori_loop(1, devices, greet, 0)
 
     for axis in range(2):
         for side in range(2):
@@ -100,15 +151,15 @@
                 lax.fori_loop(0, vectors, clear, 0)
 
     def quotient(d):
-        top = jnp.full((8, 128), aniso_ref[d, 0], jnp.int32).astype(jnp.float32)
-        return top / jnp.full((8, 128), aniso_ref[d, 1], jnp.int32).astype(jnp.float32)
+        top = jnp.full((8, 128), aniso_ref[0, d], jnp.int32).astype(jnp.float32)
+        return top / jnp.full((8, 128), aniso_ref[1, d], jnp.int32).astype(jnp.float32)
 
     coefficients = [quotient(d) for d in range(3)]
     scaled = OMEGA / (2.0 * (coefficients[0] + coefficients[1] + coefficients[2]))
     reps = (rows_y // 8, rows_z // 128)
     w = [jnp.tile(c * scaled, reps) for c in coefficients]
 
-    pl.semaphore_wait(barrier, peers)
+    pl.semaphore_wait(barrier, devices - 1)
 
     def pack(r, k):
         f = bufs[r]
@@ -117,25 +168,46 @@
             ys[r, 1, k, pl.ds(x, 1), :] = f[k, x + 1, pl.ds(0, 1), :]
 
     def send(r, k):
+        for side, source, target in ways if relayed else ():
+            @pl.when(me["gy"] == source)
+            def _():
+                for half, by in relays:
+                    to_relay(r, k, side, half, by).start()
         for axis in range(3):
             for side in range(2):
-                @pl.when(sends_to(axis, side))
+                @pl.when(direct_to(axis, side))
                 def _():
                     halo(r, k, axis, side).start()
 
     def receive(r, k):
+        forward(r, k)
         for axis in range(3):
             for side in range(2):
-                @pl.when(gets_from(axis, side))
+                @pl.when(direct_from(axis, side))
                 def _():
                     halo(r, k, axis, side).wait_recv()
+        for side, source, target in ways if relayed else ():
+            @pl.when(me["gy"] == target)
+            def _():
+                for half, by in relays:
+                    from_relay(r, k, side, half, target).wait_recv()
 
     def finish_send(r, k):
         for axis in range(3):
             for side in range(2):
-                @pl.when(sends_to(axis, side))
+                @pl.when(direct_to(axis, side))
                 def _():
                     halo(r, k, axis, side).wait_send()
+        for side, source, target in ways if relayed else ():
+            @pl.when(me["gy"] == source)
+            def _():
+                for half, by in relays:
+                    to_relay(r, k, side, half, by).wait_send()
+        for half, by in relays if relayed else ():
+            @pl.when(me["gy"] == by)
+            def _():
+                for side, source, target in ways:
+                    from_relay(r, k, side, half, target).wait_send()
 
     def first(k, _):
         load(k).wait()
@@ -167,7 +239,7 @@
             out[k, x + 1] = (1.0 - OMEGA) * c + total
             return 0
 
-        lax.fori_loop(0, rows_x, body, 0)
+        lax.fori_loop(0, rows_x, body, 0, unroll=SWEEP_UNROLL)
 
     for r in range(SWEEPS - 1):
         def step(k, _):
@@ -183,14 +255,8 @@
         lax.broadcasted_iota(jnp.int32, (256, 128), 0) // 2
         == lax.broadcasted_iota(jnp.int32, (256, 128), 1),
         0.125, 0.0,
-    )
+    ).astype(jnp.bfloat16)
     half = rows_x // 2 * rows_y
-    pair_y = jnp.where(
-        lax.broadcasted_iota(jnp.int32, (half // 2, half), 0)
-        == lax.broadcasted_iota(jnp.int32, (half // 2, half), 1) // 2,
-        1.0, 0.0,
-    )
-
     def tile_sum(product):
         parts = [
             product[i : i + 8, j : j + 128]
@@ -212,24 +278,33 @@
         finish_send(0, k)
         sweep(SWEEPS - 1, k)
         out_copy(k).start()
+        block = jnp.concatenate(
+            [
+                f0[k, 2 * x + 1, :, pl.ds(256 * j, 256)] + f0[k, 2 * x + 2, :, pl.ds(256 * j, 256)]
+                for j in range(rows_z // 256)
+                for x in range(rows_x // 2)
+            ],
+            axis=0,
+        )
+        top = block.astype(jnp.bfloat16)
+        left = block - top.astype(jnp.float32)
+        middle = left.astype(jnp.bfloat16)
+        low = (left - middle.astype(jnp.float32)).astype(jnp.bfloat16)
+        thin[...] = sum(
+            jnp.dot(piece, pair_z, preferred_element_type=jnp.float32)
+            for piece in (low, middle, top)
+        )
         for j in range(rows_z // 256):
-            block = jnp.concatenate(
-                [
-                    f0[k, 2 * x + 1, :, pl.ds(256 * j, 256)] + f0[k, 2 * x + 2, :, pl.ds(256 * j, 256)]
-                    for x in range(rows_x // 2)
-                ],
-                axis=0,
-            )
-            thin = jnp.dot(block, pair_z, precision=HIGHEST, preferred_element_type=jnp.float32)
-            mean = jnp.dot(pair_y, thin, precision=HIGHEST, preferred_element_type=jnp.float32)
-            cs[k, :, :, pl.ds(128 * j, 128)] = mean.reshape(rows_x // 2, rows_y // 2, 128)
+            even = thin[pl.ds(half * j, half // 2, stride=2), :]
+            odd = thin[pl.ds(half * j + 1, half // 2, stride=2), :]
+            cs[k, :, :, pl.ds(128 * j, 128)] = (even + odd).reshape(rows_x // 2, rows_y // 2, 128)
         coarse_copy(k).start()
 
         def pair(l, _):
             def add(x, acc):
                 return acc + tile_sum(f0[k, x + 1] * f0[l, x + 1])
 
-            acc = lax.fori_loop(0, rows_x, add, jnp.zeros((8, 128), jnp.float32))
+            acc = lax.fori_loop(0, rows_x, add, jnp.zeros((8, 128), jnp.float32), unroll=4)
             line = jnp.sum(acc, axis=0, keepdims=True)
             gp[l, pl.ds(k, 1), :] = line
             gp[k, pl.ds(l, 1), :] = line
@@ -252,38 +327,40 @@
         gram = jnp.where(lane8 == l, jnp.sum(gp[l], axis=1, keepdims=True), gram)
         gram = jnp.where(lane8 == l + 64, jnp.sum(cgp[l], axis=1, keepdims=True), gram)
 
-    for axis, name in enumerate(AXES):
-        gb = gbs[axis]
-        here = me[name]
-        gb[here] = gram
-        copies = [
-            pltpu.make_async_remote_copy(
-                src_ref=gb.at[here],
-                dst_ref=gb.at[here],
-                send_sem=gsend.at[axis, d],
-                recv_sem=grecv.at[axis, d],
-                device_id={name: lax.rem(here + d, sizes[axis])},
-                device_id_type=MESH,
-            )
-            for d in range(1, sizes[axis])
-        ]
-        for copy in copies:
-            copy.start()
-        for d in range(1, sizes[axis]):
-            source = lax.rem(here + sizes[axis] - d, sizes[axis])
-            pltpu.make_async_remote_copy(
-                src_ref=gb.at[source],
-                dst_ref=gb.at[source],
-                send_sem=gsend.at[axis, d],
-                recv_sem=grecv.at[axis, d],
-                device_id={name: lax.rem(here + d, sizes[axis])},
-                device_id_type=MESH,
-            ).wait_recv()
-        for copy in copies:
-            copy.wait_send()
-        gram = gb[0]
-        for i in range(1, sizes[axis]):
-            gram = gram + gb[i]
+    line = gram[0:1]
+    for k in range(1, vectors):
+        line = line + pltpu.roll(gram[k : k + 1], vectors * k, 1)
+    gb[here] = line
+
+    def share(d, slot):
+        return pltpu.make_async_remote_copy(
+            src_ref=gb.at[slot],
+            dst_ref=gb.at[slot],
+            send_sem=gsend.at[d],
+            recv_sem=grecv.at[d],
+            device_id=place(lax.rem(here + d, devices)),
+            device_id_type=MESH,
+        )
+
+    def share_start(d, _):
+        share(d, here).start()
+        return 0
+
+    def share_recv(d, _):
+        share(d, lax.rem(here + devices - d, devices)).wait_recv()
+        return 0
+
+    def share_sent(d, _):
+        share(d, here).wait_send()
+        return 0
+
+    lax.fori_loop(1, devices, share_start, 0)
+    lax.fori_loop(1, devices, share_recv, 0)
+    line = jnp.sum(gb[...], axis=0)
+    row8 = lax.broadcasted_iota(jnp.int32, (vectors, 128), 0)
+    gram = jnp.broadcast_to(line, (vectors, 128))
+    for k in range(1, vectors):
+        gram = jnp.where(row8 == k, pltpu.roll(line, 128 - vectors * k, 1), gram)
 
     inv_ref[...] = inverse_factor(gram / cells)
     cinv_ref[...] = inverse_factor(pltpu.roll(gram, 64, 1) / (cells // 8))
@@ -296,23 +373,26 @@
         return 0
 
     lax.fori_loop(0, vectors, drain, 0)
+    lax.fori_loop(1, devices, share_sent, 0)
 
 
 def apply_kernel(inv_ref, cinv_ref, f_ref, c_ref, b_ref, cb_ref):
     k_count = f_ref.shape[0]
 
-    def combine(factor, src, dst, columns):
-        data = [src[l, 0, :, columns] for l in range(k_count)]
+    def combine(factor, src, dst, x, columns):
+        data = [src[l, x, :, columns] for l in range(k_count)]
         for k in range(k_count):
             total = factor[k, k_count] * data[0]
             for l in range(1, k + 1):
                 total = total + factor[k, k_count + l] * data[l]
-            dst[k, 0, :, columns] = total
-
-    for j in range(0, f_ref.shape[3], 128):
-        combine(inv_ref, f_ref, b_ref, pl.ds(j, 128))
-    for j in range(0, c_ref.shape[3], 128):
-        combine(cinv_ref, c_ref, cb_ref, pl.ds(j, 128))
+            dst[k, x, :, columns] = total
+
+    for x in range(f_ref.shape[1]):
+        for j in range(0, f_ref.shape[3], 128):
+            combine(inv_ref, f_ref, b_ref, x, pl.ds(j, 128))
+    for x in range(c_ref.shape[1]):
+        for j in range(0, c_ref.shape[3], 128):
+            combine(cinv_ref, c_ref, cb_ref, x, pl.ds(j, 128))
 
 
 def local(sizes, test_vectors, aniso):
@@ -321,10 +401,11 @@
     cells = rows_x * rows_y * rows_z * sizes[0] * sizes[1] * sizes[2]
     f32 = jnp.float32
     field = pltpu.VMEM((vectors, rows_x + 2, rows_y, rows_z), f32)
-    most = max(sizes)
+    devices = sizes[0] * sizes[1] * sizes[2]
+    relayed = sizes[1] == 4 and sizes[2] == 2
     small = jax.ShapeDtypeStruct((vectors, 128), f32)
     fields, coarse, inv, cinv = pl.pallas_call(
-        functools.partial(relax_kernel, sizes, cells),
+        functools.partial(relax_kernel, sizes, cells, relayed),
         out_shape=(
             jax.ShapeDtypeStruct(test_vectors.shape, f32),
             jax.ShapeDtypeStruct(coarse_shape, f32),
@@ -345,36 +426,38 @@
             pltpu.VMEM((SWEEPS, 2, vectors, rows_x, rows_z), f32),
             pltpu.VMEM((SWEEPS, 2, vectors, rows_x, rows_z), f32),
             pltpu.VMEM((SWEEPS, 2, vectors, rows_x, rows_y, 128), f32),
+            pltpu.VMEM((SWEEPS, 2, vectors, rows_x // 2, rows_z), f32),
+            pltpu.VMEM((rows_x * rows_y * rows_z // 512, 128), f32),
             pltpu.VMEM(coarse_shape, f32),
             pltpu.VMEM((vectors, vectors, 128), f32),
             pltpu.VMEM((vectors, vectors, 128), f32),
-            *[pltpu.VMEM((n, vectors, 128), f32) for n in sizes],
+            pltpu.VMEM((devices, 1, 128), f32),
             pltpu.SemaphoreType.DMA((vectors,)),
             pltpu.SemaphoreType.DMA((vectors,)),
             pltpu.SemaphoreType.DMA((vectors,)),
             pltpu.SemaphoreType.DMA((SWEEPS, vectors, 3, 2)),
             pltpu.SemaphoreType.DMA((SWEEPS, vectors, 3, 2)),
-            pltpu.SemaphoreType.DMA((3, most)),
-            pltpu.SemaphoreType.DMA((3, most)),
+            pltpu.SemaphoreType.DMA((devices,)),
+            pltpu.SemaphoreType.DMA((devices,)),
+            *[pltpu.SemaphoreType.DMA((SWEEPS, vectors, 2))] * 4,
         ],
         compiler_params=pltpu.CompilerParams(
-            collective_id=0, has_side_effects=True, vmem_limit_bytes=60 * 2**20
+            collective_id=0, has_side_effects=True, vmem_limit_bytes=47 * 2**20
         ),
-    )(aniso, test_vectors)
-    block = pl.BlockSpec((vectors, 1, rows_y, rows_z), lambda i: (0, i, 0, 0))
-    coarse_block = pl.BlockSpec(
-        (vectors, 1, rows_y // 2, rows_z // 4), lambda i: (0, i // 2, 0, i % 2)
-    )
+    )(aniso.T, test_vectors)
+    block = pl.BlockSpec((vectors, 2, rows_y, rows_z), lambda i: (0, i, 0, 0))
+    coarse_block = pl.BlockSpec((vectors, 1, rows_y // 2, rows_z // 2), lambda i: (0, i, 0, 0))
     factor = pl.BlockSpec(memory_space=pltpu.SMEM)
     return pl.pallas_call(
         apply_kernel,
-        grid=(rows_x,),
+        grid=(rows_x // 2,),
         out_shape=(
             jax.ShapeDtypeStruct(test_vectors.shape, f32),
             jax.ShapeDtypeStruct(coarse_shape, f32),
         ),
         in_specs=[factor, factor, block, coarse_block],
         out_specs=(block, coarse_block),
+        compiler_params=pltpu.CompilerParams(vmem_limit_bytes=16 * 2**20),
     )(inv, cinv, fields, coarse)
 
 

time: 119 us -> 93 us (0.78)
  Pallas kernels: 116 us -> 88.1 us
  local copies, waits for them, and re-layouts: 1.34 us -> 4.05 us
    pallas_call x2, Pallas kernels: 116 us -> 88.1 us  [the longest x1 81.4 us: local(): pl.pallas_call(functools.partial(relax_kernel, sizes, cells, relayed), ou...]
    unnamed x1 -> x4, local copies, waits for them, and re-layouts: 1.34 us -> 4.05 us
where the time goes in v2:
time: 93 us; the launch traced here: 92.8 us
  Pallas kernels  88.1 us (95%)
  local copies, waits for them, and re-layouts  4.05 us (4%)
    pallas_call x1, Pallas kernels, local(): pl.pallas_call(functools.partial(relax_kernel, sizes, cells, relayed), ou...  81.4 us
    pallas_call x1, Pallas kernels, local(): pl.pallas_call(apply_kernel, grid=(rows_x // 2,), out_shape=(jax.ShapeDty...  6.75 us
    unnamed x4, local copies, waits for them, and re-layouts  4.05 us

profile of v2, /device:TPU:0, one launch (start us, length us, event | category | flops | bytes accessed | tf_op | source)
XLA Modules:
  0.0 92.8 jit_solution(11265909945556922806)
XLA Ops:
  0.6 0.0 copy-start.1
  0.6 0.7 copy-done.1
  1.3 81.4 %shard_map.41 = (f32[8,16,16,1024]{3,2,1,0:T(8,128)}, f32[8,8,8,512]{3,2,1,0:T(8,128)S(1)}, f32[8,128]{1,0:T(8,128)S(1)}, f32[8,128]{1,0:T(8,128)S(1)}) custom-call(s32[2,3]{1,0:T(2,128)S(1)} %bitcast.1, f32[8,16,16,1024]{3,2,1,0:T(8,128)} %v_ref.1), custom_call_target="tpu_custom_call" | custom-call | tf_op jit(solution)/shard_map/pallas_call | solution.py:407
  82.7 0.0 copy-start
  82.7 3.4 %copy-done = f32[8,16,16,1024]{3,2,1,0:T(8,128)S(1)} copy-done((f32[8,16,16,1024]{3,2,1,0:T(8,128)S(1)}, f32[8,16,16,1024]{3,2,1,0:T(8,128)}, u32[]{:S(2)}) %copy-start) | copy-done | bytes 8388632
  86.1 6.7 %shard_map.42 = (f32[8,16,16,1024]{3,2,1,0:T(8,128)}, f32[8,8,8,512]{3,2,1,0:T(8,128)}) custom-call(f32[8,128]{1,0:T(8,128)S(1)} %get-tuple-element.6.inv_ref, f32[8,128]{1,0:T(8,128)S(1)} %get-tuple-element.7.cinv_ref, f32[8,16,16,1024]{3,2,1,0:T(8,128)S(1)} %copy-done, f32[8,8,8,512]{3,2,1,0:T(8,128)S(1)} %get-tuple-element.9.c_ref), custom_call_target="tpu_custom_call" | custom-call | tf_op jit(solution)/shard_map/pallas_call | solution.py:451
Async XLA Ops:
  0.6 0.7 copy-start.1
  82.7 3.4 %copy-start = (f32[8,16,16,1024]{3,2,1,0:T(8,128)S(1)}, f32[8,16,16,1024]{3,2,1,0:T(8,128)}, u32[]{:S(2)}) copy-start(f32[8,16,16,1024]{3,2,1,0:T(8,128)} %get-tuple-element.8.f_ref) | copy-start | bytes 25165828

commit v3 on v2

--- a/solution.py
+++ b/solution.py
@@ -388,8 +388,8 @@
             dst[k, x, :, columns] = total
 
     for x in range(f_ref.shape[1]):
-        for j in range(0, f_ref.shape[3], 128):
-            combine(inv_ref, f_ref, b_ref, x, pl.ds(j, 128))
+        for j in range(0, f_ref.shape[3], 256):
+            combine(inv_ref, f_ref, b_ref, x, pl.ds(j, 256))
     for x in range(c_ref.shape[1]):
         for j in range(0, c_ref.shape[3], 128):
             combine(cinv_ref, c_ref, cb_ref, x, pl.ds(j, 128))
@@ -442,22 +442,22 @@
             *[pltpu.SemaphoreType.DMA((SWEEPS, vectors, 2))] * 4,
         ],
         compiler_params=pltpu.CompilerParams(
-            collective_id=0, has_side_effects=True, vmem_limit_bytes=47 * 2**20
+            collective_id=0, has_side_effects=True, vmem_limit_bytes=60 * 2**20
         ),
     )(aniso.T, test_vectors)
-    block = pl.BlockSpec((vectors, 2, rows_y, rows_z), lambda i: (0, i, 0, 0))
-    coarse_block = pl.BlockSpec((vectors, 1, rows_y // 2, rows_z // 2), lambda i: (0, i, 0, 0))
+    block = pl.BlockSpec((vectors, 4, rows_y, rows_z), lambda i: (0, i, 0, 0))
+    coarse_block = pl.BlockSpec((vectors, 2, rows_y // 2, rows_z // 2), lambda i: (0, i, 0, 0))
     factor = pl.BlockSpec(memory_space=pltpu.SMEM)
     return pl.pallas_call(
         apply_kernel,
-        grid=(rows_x // 2,),
+        grid=(rows_x // 4,),
         out_shape=(
             jax.ShapeDtypeStruct(test_vectors.shape, f32),
             jax.ShapeDtypeStruct(coarse_shape, f32),
         ),
         in_specs=[factor, factor, block, coarse_block],
         out_specs=(block, coarse_block),
-        compiler_params=pltpu.CompilerParams(vmem_limit_bytes=16 * 2**20),
+        compiler_params=pltpu.CompilerParams(vmem_limit_bytes=60 * 2**20),
     )(inv, cinv, fields, coarse)
 
 

time: 93 us -> 90.1 us (0.969)
  local copies, waits for them, and re-layouts: 4.05 us -> 0 us
  Pallas kernels: 88.1 us -> 89.3 us
    unnamed x4 -> x0, local copies, waits for them, and re-layouts: 4.05 us -> none
    pallas_call x1, Pallas kernels: 6.75 us -> 8.44 us  [local(): pl.pallas_call(apply_kernel, grid=(rows_x // 4,), out_shape=(jax.ShapeDty...]
where the time goes in v3:
time: 90.1 us; the launch traced here: 89.9 us
  Pallas kernels  89.3 us (99%)
    pallas_call x1, Pallas kernels, local(): pl.pallas_call(functools.partial(relax_kernel, sizes, cells, relayed), ou...  80.9 us
    pallas_call x1, Pallas kernels, local(): pl.pallas_call(apply_kernel, grid=(rows_x // 4,), out_shape=(jax.ShapeDty...  8.44 us

profile of v3, /device:TPU:0, one launch (start us, length us, event | category | flops | bytes accessed | tf_op | source)
XLA Modules:
  0.0 89.9 jit_solution(10605763984818037298)
XLA Ops:
  0.6 80.9 %shard_map.41 = (f32[8,16,16,1024]{3,2,1,0:T(8,128)}, f32[8,8,8,512]{3,2,1,0:T(8,128)}, f32[8,128]{1,0:T(8,128)}, f32[8,128]{1,0:T(8,128)}) custom-call(s32[2,3]{1,0:T(2,128)} %bitcast.1, f32[8,16,16,1024]{3,2,1,0:T(8,128)} %v_ref.1), custom_call_target="tpu_custom_call" | custom-call | tf_op jit(solution)/shard_map/pallas_call | solution.py:407
  81.5 8.4 %shard_map.42 = (f32[8,16,16,1024]{3,2,1,0:T(8,128)}, f32[8,8,8,512]{3,2,1,0:T(8,128)}) custom-call(f32[8,128]{1,0:T(8,128)} %get-tuple-element.6.inv_ref, f32[8,128]{1,0:T(8,128)} %get-tuple-element.7.cinv_ref, f32[8,16,16,1024]{3,2,1,0:T(8,128)} %get-tuple-element.8.f_ref, f32[8,8,8,512]{3,2,1,0:T(8,128)} %get-tuple-element.9.c_ref), custom_call_target="tpu_custom_call" | custom-call | tf_op jit(solution)/shard_map/pallas_call | solution.py:451
